TPU v7x, 128 devices: a whole 4x4x4 slice. The times are simulated.
128 devices in a mesh: grp: 4 (over z), tile: 32 (over x, y, core).
Axes of the slice: x: 4, y: 4, z: 4, core: 2. Of those that a mesh axis runs over, the one named last changes fastest.
Arguments:
- noise: bfloat16 [16, 3, 2048, 2048], P('grp', None, 'tile'), may hold values from -6 to 6
- stress: float32 [6, 2048, 2048], P(None, 'tile', 'grp'), as said below
- timescale: float32 [2048, 2048], P('tile', 'grp'), may hold values from 3 to 256
- mean_inflow: float32 [2048, 2048], P('tile', 'grp'), may hold values from 0.5 to 1.5
- courant: float32 [2048, 2048], P('tile', 'grp'), may hold values from 0.2 to 0.9
- prior_state: float32 [3, 2048, 2048], P(None, 'tile', 'grp'), may hold values from -6 to 6
- field: float32 [3, 8, 2048, 2048], P(None, None, 'tile', 'grp'), may hold values from -6 to 6
Outputs:
- inflow: bfloat16 [16, 3, 2048, 2048], P(None, None, 'tile', 'grp')
- field_out: float32 [3, 8, 2048, 2048], P(None, None, 'tile', 'grp')
Inputs may be any that keep to these rules, and one draw needn't show every extreme that they name: stress holds, per cell, R11, R21, R22, R31, R32, R33 of a symmetric positive definite tensor whose Cholesky factor has diagonal entries of 0.3 or more.
All inputs are finite; a program needn't handle non-finite values.
Results may differ from a plain program's by a relative error of at most 0.0085.
Values may be sent and summed in bfloat16 or wider, within the bound.
No kernel may reach another device: no remote copies, remote signals or barrier semaphores. Data moves between devices by JAX's collectives and lax.ppermute only.
A program may use at most 128 MiB of HBM per device.

v0:
```python
import math

import jax
import jax.numpy as jnp
from jax import lax
from jax.sharding import PartitionSpec as P

LS = 2
FW = 4


def padded_2(value, sides, width, wrap):
    for axis, dim in sides:
        devices, length = (lax.axis_size(axis), value.shape[dim])
        up = [(i, (i + 1) % devices) for i in range(devices if wrap else devices - 1)]
        down = [(j, i) for i, j in up]
        last = lax.slice_in_dim(value, length - width, length, axis=dim)
        initial = lax.slice_in_dim(value, 0, width, axis=dim)
        before = lax.ppermute(last, axis, up)
        after = lax.ppermute(initial, axis, down)
        value = jnp.concatenate([before, value, after], axis=dim)
    return value


def filter_taps():
    offsets = jnp.arange(-FW, FW + 1).astype(jnp.float32)
    raw = jnp.exp(-math.pi * offsets * offsets / (2.0 * LS * LS))
    return (raw / jnp.sqrt(jnp.sum(raw * raw))).astype(jnp.bfloat16)


def band_matrix(rows, taps):
    width = taps.shape[0]
    distance = jnp.arange(rows + width - 1)[None, :] - jnp.arange(rows)[:, None]
    picks = distance[:, :, None] == jnp.arange(width)[None, None, :]
    return jnp.sum(jnp.where(picks, taps.astype(jnp.float32), 0.0), axis=2).astype(jnp.bfloat16)


def filter_last(padded, taps):
    width = taps.shape[0]
    length = padded.shape[-1] - width + 1
    block = math.gcd(length, 128)
    weights = band_matrix(block, taps)
    windows = jnp.stack(
        [
            lax.slice_in_dim(padded, start, start + block + width - 1, axis=padded.ndim - 1)
            for start in range(0, length, block)
        ],
        axis=-2,
    )
    result = jnp.einsum("...kw,bw->...kb", windows, weights, preferred_element_type=jnp.float32)
    return result.reshape(result.shape[:-2] + (length,))


def filter_rows(padded, taps):
    rows = padded.shape[2] - taps.shape[0] + 1
    weights = band_matrix(rows, taps)
    return jnp.einsum("ij,pcjz->pciz", weights, padded, preferred_element_type=jnp.float32)


def cholesky_cells(stress):
    first_diag = jnp.sqrt(stress[0])
    second_low = stress[1] / first_diag
    second_diag = jnp.sqrt(stress[2] - second_low * second_low)
    third_low = stress[3] / first_diag
    third_mid = (stress[4] - second_low * third_low) / second_diag
    third_diag = jnp.sqrt(stress[5] - third_low * third_low - third_mid * third_mid)
    return (first_diag, second_low, second_diag, third_low, third_mid, third_diag)


def velocity_of(state, factors, mean_inflow):
    first_diag, second_low, second_diag, third_low, third_mid, third_diag = factors
    return jnp.stack(
        [
            mean_inflow + first_diag * state[0],
            second_low * state[0] + second_diag * state[1],
            third_low * state[0] + third_mid * state[1] + third_diag * state[2],
        ]
    )


def march(current, courant, velocity):
    upstream = jnp.concatenate([velocity[:, None], current[:, :-1]], axis=1)
    return (1.0 - courant) * current + courant * upstream


def tile_chain(filtered, stress, timescale, mean_inflow, courant, prior_state, field):
    decay = jnp.exp(-math.pi / (2.0 * timescale))
    gain = jnp.sqrt(1.0 - decay * decay)
    factors = cholesky_cells(stress)

    def advance(carry, plane):
        state, current = carry
        state = decay * state + gain * plane
        velocity = velocity_of(state, factors, mean_inflow)
        return ((state, march(current, courant, velocity)), velocity.astype(jnp.bfloat16))

    (state, result), inflow = lax.scan(advance, (prior_state, field), filtered)
    return (inflow, result)


def body(noise, stress, timescale, mean_inflow, courant, prior_state, field):
    taps = filter_taps()
    flipped = jnp.swapaxes(noise, 2, 3)
    tiles = lax.all_to_all(
        lax.all_to_all(flipped, "tile", split_axis=2, concat_axis=3, tiled=True),
        "grp",
        split_axis=3,
        concat_axis=0,
        tiled=True,
    )
    banded = padded_2(tiles, (("grp", 3),), FW, False)
    widened = padded_2(banded, (("tile", 2),), FW, True)
    span = filter_rows(widened, taps).astype(jnp.bfloat16)
    filtered = filter_last(span, taps)
    inflow, result = tile_chain(
        filtered, stress, timescale, mean_inflow, courant, prior_state, field
    )
    return (inflow, result)


def solution(mesh):
    placed = (
        P("grp", None, "tile", None),
        P(None, "tile", "grp"),
        P("tile", "grp"),
        P("tile", "grp"),
        P("tile", "grp"),
        P(None, "tile", "grp"),
        P(None, None, "tile", "grp"),
    )
    return jax.shard_map(
        body,
        mesh=mesh,
        in_specs=placed,
        out_specs=(P(None, None, "tile", "grp"), P(None, None, "tile", "grp")),
        check_vma=False,
    )
```

profile of v0, /device:TPU:1, one launch (start us, length us, event | category | flops | bytes accessed | tf_op | source)
XLA Modules:
  0.0 307.2 jit_solution(12647594609920412347)
XLA Ops:
  0.6 1.9 copy-done.7
  2.5 7.1 %copy.41 = bf16[4,3,64,2048]{2,0,1,3:T(4,128)(2,1)} copy(bf16[4,3,64,2048]{3,2,1,0:T(8,128)(2,1)S(1)} %copy-done.7) | data formatting | bytes 6291456 | tf_op args[0]
  9.6 7.7 %bitcast_bitcast_fusion = bf16[2048,3,4,64]{3,2,1,0:T(4,128)(2,1)} fusion(bf16[4,3,64,2048]{2,0,1,3:T(4,128)(2,1)} %copy.41), kind=kLoop, calls=%fused_computation.73 | loop fusion | bytes 6291456
  17.3 7.5 %reshape.107 = bf16[32,2,24576]{2,1,0:T(2,128)(2,1)S(1)} reshape(bf16[2048,3,4,64]{3,2,1,0:T(4,128)(2,1)} %bitcast_bitcast_fusion) | data formatting | bytes 6291456
  24.8 47.9 %all_to_all.36 = bf16[32,2,24576]{2,1,0:T(2,128)(2,1)} all-to-all(bf16[32,2,24576]{2,1,0:T(2,128)(2,1)S(1)} %reshape.107), channel_id=1, replica_groups=mesh['grp'=4,'tile'=32] {'tile'}, dimensions={0} | all-to-all | bytes 6291456 | tf_op jit(solution)/shard_map/all_to_all | solution.py:105
  72.7 8.7 %reshape.108 = bf16[2048,3,4,64]{3,2,1,0:T(4,128)(2,1)} reshape(bf16[32,2,24576]{2,1,0:T(2,128)(2,1)} %all_to_all.36) | data formatting | bytes 6291456
  81.4 9.5 %copy.65 = bf16[4,3,32,64,64]{4,2,3,1,0:T(8,128)(2,1)} copy(bf16[4,3,32,64,64]{4,0,1,3,2:T(4,128)(2,1)} %bitcast.127) | data formatting | bytes 6291456 | tf_op jit(solution)/shard_map/all_to_all | solution.py:105
  90.9 11.8 %copy.54 = bf16[4,3,64,32,64]{2,0,1,4,3:T(4,128)(2,1)} copy(bf16[4,3,64,32,64]{4,3,2,1,0:T(8,128)(2,1)} %bitcast.128) | data formatting | bytes 6291456 | tf_op jit(solution)/shard_map/all_to_all | solution.py:105
  102.7 7.7 %reshape.109 = bf16[4,2,196608]{2,1,0:T(2,128)(2,1)} reshape(bf16[2048,3,4,64]{3,2,1,0:T(4,128)(2,1)} %bitcast.129) | data formatting | bytes 6291456
  110.4 5.2 %all-to-all-start.1 = ((bf16[4,2,196608]{2,1,0:T(2,128)(2,1)}), bf16[4,2,196608]{2,1,0:T(2,128)(2,1)S(1)}, u32[]{:S(2)}, u32[]{:S(2)}) async-start(bf16[4,2,196608]{2,1,0:T(2,128)(2,1)} %reshape.109), calls=%async_computation.1 | async-start | bytes 6291456 | tf_op jit(solution)/shard_map/all_to_all | solution.py:104
  117.1 2.2 fusion.24
  119.9 1.6 fusion.26
  121.5 31.4 %all-to-all-done.1 = bf16[4,2,196608]{2,1,0:T(2,128)(2,1)S(1)} async-done(((bf16[4,2,196608]{2,1,0:T(2,128)(2,1)}), bf16[4,2,196608]{2,1,0:T(2,128)(2,1)S(1)}, u32[]{:S(2)}, u32[]{:S(2)}) %all-to-all-start.1) | async-done | bytes 3145760 | tf_op jit(solution)/shard_map/all_to_all | solution.py:104
  152.9 5.3 %reshape.110 = bf16[2048,3,4,64]{3,2,1,0:T(4,128)(2,1)} reshape(bf16[4,2,196608]{2,1,0:T(2,128)(2,1)S(1)} %all-to-all-done.1) | data formatting | bytes 6291456
  158.2 8.3 %copy.45 = bf16[4,4,3,64,512]{4,3,2,1,0:T(8,128)(2,1)S(1)} copy(bf16[4,4,3,64,512]{3,1,2,4,0:T(4,128)(2,1)} %bitcast.130) | data formatting | bytes 6291456 | tf_op jit(solution)/shard_map/all_to_all | solution.py:104
  166.4 1.5 fusion.38
  168.0 1.5 copy.46
  169.5 1.5 copy.47
  172.3 4.2 %collective-permute-start = (bf16[16,3,64,4]{2,0,3,1:T(8,128)(2,1)S(1)}, bf16[16,3,64,4]{2,0,3,1:T(8,128)(2,1)S(1)}, u32[]{:S(2)}, u32[]{:S(2)}) collective-permute-start(bf16[16,3,64,4]{2,0,3,1:T(8,128)(2,1)S(1)} %copy.46), channel_id=1, source_target_pairs={{0,32},{32,64},{64,96},{1,33},{33,65},{65,97},{2,34},{34,66},{66,9... | collective-permute-start | bytes 73736 | tf_op jit(solution)/shard_map/ppermute | solution.py:19
  180.0 1.8 pad_maximum_fusion.3
  181.8 1.9 collective-permute-start.2
  184.3 1.6 sqrt_bitcast_fusion
  186.8 2.5 collective-permute-done.3
  189.3 4.2 %convert_bitcast_fusion.3 = bf16[16,3,64,520]{3,2,1,0:T(8,128)(2,1)S(1)} fusion(bf16[16,3,4,520]{3,2,1,0:T(4,128)(2,1)S(1)} %collective-permute-done.3, bf16[16,3,64,4]{3,2,1,0:T(8,128)(2,1)S(1)} %copy-done.6, bf16[16,3,64,512]{3,2,1,0:T(8,128)(2,1)S(1)} %bitcast.133, bf16[16,3,64,4]{3,2,1,0:T(8,128)(2,1)S(1)} %copy-done.5, ...), kind=kOutput, calls=%fused_computation.35 | convolution fusion | flops 249600000 | bytes 6798336 | tf_op jit(solution)/shard_map/ij,pcjz->pciz/dot_general | solution.py:57
  194.4 2.6 fusion.18
  197.0 3.5 %copy.64 = f32[16,3,4,8,8,128]{5,4,2,3,1,0:T(8,128)} copy(f32[16,3,4,8,8,128]{5,4,3,2,1,0:T(8,128)S(1)} %fusion.18) | data formatting | bytes 12582912 | tf_op jit(solution)/shard_map/reshape | solution.py:51
  200.4 105.1 %while.14 = (s32[]{:T(128)}, f32[3,64,512]{2,1,0:T(8,128)S(1)}, f32[3,8,64,512]{3,2,1,0:T(8,128)S(1)}, bf16[16,3,64,512]{3,2,1,0:T(8,128)(2,1)}, f32[64,512]{1,0...) while((s32[]{:T(128)}, f32[3,64,512]{2,1,0:T(8,128)S(1)}, ...), condition=%wide.region_4.5_spmd, body=%wide.region_3.4_spmd.sunk | while | flops 4685826 | bytes 20512960 | solution.py:97
  202.6 1.4 convert_bitcast_fusion.5
  209.2 1.4 convert_bitcast_fusion.5
  215.8 1.4 convert_bitcast_fusion.5
  222.3 1.4 convert_bitcast_fusion.5
  305.6 1.7 copy-done
  (169 shorter events, 107.7 us)
Async XLA Ops:
  0.6 1.9 copy-start.7
  110.4 6.7 %copy-start.8 = (f32[64,512]{1,0:T(8,128)S(1)}, f32[64,512]{1,0:T(8,128)}, u32[]{:S(2)}) copy-start(f32[64,512]{1,0:T(8,128)} %param.11) | copy-start | bytes 393220
  110.4 42.4 %all-to-all-start.1 = ((bf16[4,2,196608]{2,1,0:T(2,128)(2,1)}), bf16[4,2,196608]{2,1,0:T(2,128)(2,1)S(1)}, u32[]{:S(2)}, u32[]{:S(2)}) async-start(bf16[4,2,196608]{2,1,0:T(2,128)(2,1)} %reshape.109), calls=%async_computation.1 | async-start | bytes 6291456 | tf_op jit(solution)/shard_map/all_to_all | solution.py:104
  119.2 0.7 copy-start.4
  171.0 7.7 %collective-permute-start.1 = (bf16[16,3,64,4]{2,0,3,1:T(8,128)(2,1)S(1)}, bf16[16,3,64,4]{2,0,3,1:T(8,128)(2,1)S(1)}, u32[]{:S(2)}, u32[]{:S(2)}) collective-permute-start(bf16[16,3,64,4]{2,0,3,1:T(8,128)(2,1)S(1)} %copy.47), channel_id=1, source_target_pairs={{32,0},{64,32},{96,64},{33,1},{65,33},{97,65},{34,2},{66,34},{98,6... | collective-permute-start | bytes 73736 | tf_op jit(solution)/shard_map/ppermute | solution.py:20
  172.3 5.2 %collective-permute-start = (bf16[16,3,64,4]{2,0,3,1:T(8,128)(2,1)S(1)}, bf16[16,3,64,4]{2,0,3,1:T(8,128)(2,1)S(1)}, u32[]{:S(2)}, u32[]{:S(2)}) collective-permute-start(bf16[16,3,64,4]{2,0,3,1:T(8,128)(2,1)S(1)} %copy.46), channel_id=1, source_target_pairs={{0,32},{32,64},{64,96},{1,33},{33,65},{65,97},{2,34},{34,66},{66,9... | collective-permute-start | bytes 73736 | tf_op jit(solution)/shard_map/ppermute | solution.py:19
  180.0 9.3 %copy-start.5 = (bf16[16,3,64,4]{3,2,1,0:T(8,128)(2,1)S(1)}, bf16[16,3,64,4]{3,2,1,0:T(8,128)(2,1)}, u32[]{:S(2)}) copy-start(bf16[16,3,64,4]{3,2,1,0:T(8,128)(2,1)} %copy.48) | copy-start | bytes 73732
  180.0 9.3 %copy-start.6 = (bf16[16,3,64,4]{3,2,1,0:T(8,128)(2,1)S(1)}, bf16[16,3,64,4]{3,2,1,0:T(8,128)(2,1)}, u32[]{:S(2)}) copy-start(bf16[16,3,64,4]{3,2,1,0:T(8,128)(2,1)} %copy.49) | copy-start | bytes 73732
  181.8 5.0 %collective-permute-start.2 = (bf16[16,3,4,520]{3,2,1,0:T(4,128)(2,1)S(1)}, bf16[16,3,4,520]{3,2,1,0:T(4,128)(2,1)S(1)}, u32[]{:S(2)}, u32[]{:S(2)}) collective-permute-start(bf16[16,3,4,520]{3,2,1,0:T(4,128)(2,1)S(1)} %get-tuple-element.126), channel_id=1, source_target_pairs={{0,1},{1,2},{2,3},{3,4},{4,5},{5,6},{6,7},{7,8},{8,9},{9,10},{10,1... | collective-permute-start | bytes 599048 | tf_op jit(solution)/shard_map/ppermute | solution.py:19
  183.7 5.6 %collective-permute-start.3 = (bf16[16,3,4,520]{3,2,1,0:T(4,128)(2,1)S(1)}, bf16[16,3,4,520]{3,2,1,0:T(4,128)(2,1)S(1)}, u32[]{:S(2)}, u32[]{:S(2)}) collective-permute-start(bf16[16,3,4,520]{3,2,1,0:T(4,128)(2,1)S(1)} %get-tuple-element.127), channel_id=1, source_target_pairs={{1,0},{2,1},{3,2},{4,3},{5,4},{6,5},{7,6},{8,7},{9,8},{10,9},{11,1... | collective-permute-start | bytes 599048 | tf_op jit(solution)/shard_map/ppermute | solution.py:20
  196.9 3.5 %copy-start.1 = (f32[3,8,64,512]{3,2,1,0:T(8,128)S(1)}, f32[3,8,64,512]{3,2,1,0:T(8,128)}, u32[]{:S(2)}) copy-start(f32[3,8,64,512]{3,2,1,0:T(8,128)} %param.15) | copy-start | bytes 9437188
  197.0 3.5 %copy-start.2 = (f32[3,64,512]{2,1,0:T(8,128)S(1)}, f32[3,64,512]{2,1,0:T(8,128)}, u32[]{:S(2)}) copy-start(f32[3,64,512]{2,1,0:T(8,128)} %param.14) | copy-start | bytes 1179652
  204.0 0.9 copy-start.3
  210.6 0.9 copy-start.3
  217.2 0.9 copy-start.3
  223.7 0.9 copy-start.3
  230.3 0.9 copy-start.3
  236.9 0.9 copy-start.3
  243.4 0.9 copy-start.3
  250.0 0.9 copy-start.3
  256.6 0.9 copy-start.3
  263.1 0.9 copy-start.3
  269.7 0.9 copy-start.3
  276.3 0.9 copy-start.3
  282.9 0.9 copy-start.3
  289.4 0.9 copy-start.3
  296.0 0.9 copy-start.3
  302.6 0.9 copy-start.3
  305.6 1.7 copy-start
where the time goes:
time: 313 us; the launch traced here: 307 us
  local copies, waits for them, and re-layouts  105 us (34%)
  other arithmetic  97.3 us (31%)
  blocking collectives  47.9 us (15%)
  waiting for transfers between devices  35.6 us (11%)
  starting transfers between devices  13.2 us (4%)
  matrix products  6.73 us (2%)
    unnamed x22, local copies, waits for them, and re-layouts  48.3 us
    all_to_all x1, blocking collectives, body(): lax.all_to_all(flipped, 'tile', split_axis=2, concat_axis=3, tiled=True)  47.9 us
    all_to_all x1, waiting for transfers between devices, body(): lax.all_to_all(lax.all_to_all(flipped, 'tile', split_axis=2, concat_axis=...  31.4 us
    another operation x16, other arithmetic, velocity_of(): jnp.stack([mean_inflow + first_diag * state[0], second_low * state[0] + s...  22.1 us
    add x16, other arithmetic, march(): return (1.0 - courant) * current + courant * upstream  22.1 us
    all_to_all x2, local copies, waits for them, and re-layouts, body(): lax.all_to_all(flipped, 'tile', split_axis=2, concat_axis=3, tiled=True)  21.3 us
    add x16, other arithmetic, advance(): state = decay * state + gain * plane  20.4 us
    sub x16, other arithmetic, march(): return (1.0 - courant) * current + courant * upstream  14.6 us
  transfers between devices with their start and end apart: 5, of which 4 were waited for; matrix products, arithmetic and copies ran while one was open for 2% of the time, Pallas kernels for 0%

commit v1 on v0

v1 whole, which is shorter than its diff:
```python
import math

import jax
import jax.numpy as jnp
import ml_dtypes
import numpy as np
from jax import lax
from jax.experimental import pallas as pl
from jax.experimental.pallas import tpu as pltpu
from jax.sharding import PartitionSpec as P

LS = 2
FW = 4
TAPS = 2 * FW + 1
CX = 8
BF16 = jnp.bfloat16
F32 = jnp.float32


def filter_taps():
    offsets = np.arange(-FW, FW + 1, dtype=np.float32)
    raw = np.exp(-math.pi * offsets * offsets / (2.0 * LS * LS)).astype(np.float32)
    return (raw / np.sqrt(np.sum(raw * raw))).astype(ml_dtypes.bfloat16)


def pick(taps, index):
    inside = (index >= 0) & (index < TAPS)
    return np.where(inside, taps.astype(np.float32)[np.clip(index, 0, TAPS - 1)], 0.0)


def filter_weights(planes, rows):
    taps = filter_taps()
    span = pick(taps, np.arange(256)[None, :] - np.arange(128)[:, None] - 64 + FW)
    row = np.arange(rows)
    one = pick(taps, row[:, None] - row[None, :] + FW)
    quad = np.zeros((4 * rows, 4 * rows), np.float32)
    for q in range(4):
        quad[q * rows : (q + 1) * rows, q * rows : (q + 1) * rows] = one
    outer = np.concatenate([np.arange(FW) - FW, rows + np.arange(FW)])
    edge = pick(taps, outer[:, None] - row[None, :] + FW)
    halo = np.zeros((planes // 4, planes * 2 * FW, 4 * rows), np.float32)
    for m in range(planes):
        j, q = divmod(m, 4)
        halo[j, m * 2 * FW : (m + 1) * 2 * FW, q * rows : (q + 1) * rows] = edge
    cast = lambda a: jnp.asarray(a.astype(ml_dtypes.bfloat16))
    return cast(span), cast(quad), cast(halo)


def filter_kernel(left_ref, right_ref, hleft_ref, hright_ref, span_ref, quad_ref, halo_ref, out_ref):
    w = pl.program_id(0)
    planes, rows, lanes = left_ref.shape
    blocks = out_ref.shape[0]
    turned = (((1,), (1,)), ((), ()))
    window = jnp.concatenate([left_ref[...], right_ref[...]], axis=-1).reshape(planes * rows, 2 * lanes)
    edges = jnp.concatenate([hleft_ref[...], hright_ref[...]], axis=-1)
    band = span_ref[...]
    main = lax.dot_general(band, window, turned, preferred_element_type=F32).astype(BF16)
    edge = lax.dot_general(band, edges, turned, preferred_element_type=F32).astype(BF16)
    for j in range(planes // 4):
        part = jnp.dot(main[:, 4 * rows * j : 4 * rows * (j + 1)], quad_ref[...], preferred_element_type=F32)
        part += jnp.dot(edge, halo_ref[j], preferred_element_type=F32)
        part = part.astype(BF16)
        for h in range(2):
            t = lax.rem(2 * w + 1 + h, blocks)
            for k in range(2):
                out_ref[t, 2 * j + k] = part[64 * h : 64 * (h + 1), 128 * k : 128 * (k + 1)]


def filter_planes(noise, halo, weights):
    planes, rows, length = noise.shape
    windows = length // 128
    span, quad, edge = weights
    whole = lambda a: pl.BlockSpec(a.shape, lambda w: (0,) * a.ndim)
    return pl.pallas_call(
        filter_kernel,
        grid=(windows,),
        in_specs=[
            pl.BlockSpec((planes, rows, 128), lambda w: (0, 0, w)),
            pl.BlockSpec((planes, rows, 128), lambda w: (0, 0, lax.rem(w + 1, windows))),
            pl.BlockSpec((halo.shape[0], 128), lambda w: (0, w)),
            pl.BlockSpec((halo.shape[0], 128), lambda w: (0, lax.rem(w + 1, windows))),
            whole(span),
            whole(quad),
            whole(edge),
        ],
        out_specs=pl.BlockSpec((2 * windows, planes // 2, 64, 2 * rows), lambda w: (0, 0, 0, 0)),
        out_shape=jax.ShapeDtypeStruct((2 * windows, planes // 2, 64, 2 * rows), BF16),
        compiler_params=pltpu.CompilerParams(vmem_limit_bytes=40 * 2**20),
        name="filter",
    )(noise, noise, halo, halo, span, quad, edge)


def chain_kernel(
    got_ref, stress_ref, timescale_ref, mean_ref, courant_ref, prior_ref, field_ref, inflow_ref, result_ref, vel_ref
):
    groups, bands = got_ref.shape[:2]
    pairs = got_ref.shape[3]
    depth = got_ref.shape[4]
    per = 2 * pairs // 3
    steps = groups * per
    low = lax.broadcasted_iota(jnp.int32, (depth, 128), 1) < 64

    def band(b, _):
        lanes = pl.ds(pl.multiple_of(b * 128, 128), 128)
        courant = courant_ref[:, lanes]
        rest = 1.0 - courant
        inverse = 1.0 / rest
        decay = jnp.exp(-math.pi / (2.0 * timescale_ref[:, lanes]))
        gain = jnp.sqrt(1.0 - decay * decay)
        first = jnp.sqrt(stress_ref[0, :, lanes])
        second_low = stress_ref[1, :, lanes] / first
        second = jnp.sqrt(stress_ref[2, :, lanes] - second_low * second_low)
        third_low = stress_ref[3, :, lanes] / first
        third_mid = (stress_ref[4, :, lanes] - second_low * third_low) / second
        third = jnp.sqrt(stress_ref[5, :, lanes] - third_low * third_low - third_mid * third_mid)
        first, second_low, second = first * gain, second_low * gain, second * gain
        third_low, third_mid, third = third_low * gain, third_mid * gain, third * gain
        mean = mean_ref[:, lanes]
        phi = [prior_ref[m, :, lanes] / gain for m in range(3)]
        scale = courant * inverse
        for g in range(groups):
            planes = []
            for k in range(pairs):
                one = got_ref[g, b, 0, k].astype(F32)
                two = got_ref[g, b, 1, k].astype(F32)
                planes.append(jnp.where(low, one, pltpu.roll(two, 64, 1)))
                planes.append(jnp.where(low, pltpu.roll(one, 64, 1), two))
            for i in range(per):
                p = g * per + i
                phi = [decay * phi[m] + planes[3 * i + m] for m in range(3)]
                vel = (
                    mean + first * phi[0],
                    second_low * phi[0] + second * phi[1],
                    third_low * phi[0] + third_mid * phi[1] + third * phi[2],
                )
                for m in range(3):
                    inflow_ref[p, m, :, lanes] = vel[m].astype(BF16)
                    vel_ref[p, m] = vel[m] * scale
                scale = scale * inverse
        ratio = courant * inverse
        back = rest / courant
        square = rest * rest
        square = square * square
        square = square * square
        last = square * square
        for m in range(3):
            power = None
            cells = []
            for x in range(CX):
                start = field_ref[m, x, :, lanes]
                cells.append(start if x == 0 else start * power)
                power = back if x == 0 else power * back
            for p in range(steps):
                inlet = vel_ref[p, m]
                cells = [cells[x] + (inlet if x == 0 else cells[x - 1]) for x in range(CX)]
            power = last
            for x in range(CX):
                result_ref[m, x, :, lanes] = cells[x] * power
                power = power * ratio
        return _

    lax.fori_loop(0, bands, band, 0)


def march_cells(got, stress, timescale, mean, courant, prior, field):
    groups, bands, cores, pairs, depth, wide = got.shape
    rows = 16
    length = timescale.shape[1]
    steps = groups * 2 * pairs // 3
    spec = lambda *lead: pl.BlockSpec(lead + (rows, length), lambda s: (0,) * len(lead) + (s, 0))
    return pl.pallas_call(
        chain_kernel,
        grid=(depth // rows,),
        in_specs=[
            pl.BlockSpec((groups, bands, cores, pairs, rows, wide), lambda s: (0, 0, 0, 0, s, 0)),
            spec(6),
            spec(),
            spec(),
            spec(),
            spec(3),
            spec(3, CX),
        ],
        out_specs=[spec(steps, 3), spec(3, CX)],
        out_shape=[
            jax.ShapeDtypeStruct((steps, 3, depth, length), BF16),
            jax.ShapeDtypeStruct((3, CX, depth, length), F32),
        ],
        scratch_shapes=[pltpu.VMEM((steps, 3, rows, 128), F32)],
        compiler_params=pltpu.CompilerParams(vmem_limit_bytes=40 * 2**20),
        name="march",
    )(got, stress, timescale, mean, courant, prior, field)


def body(noise, stress, timescale, mean_inflow, courant, prior_state, field):
    per, comps, rows, length = noise.shape
    planes = per * comps
    tiles, groups = lax.axis_size("tile"), lax.axis_size("grp")
    noise = noise.reshape(planes, rows, length)
    up = [(i, i + 1) for i in range(tiles - 1)]
    down = [(i + 1, i) for i in range(tiles - 1)]
    before = lax.ppermute(noise[:, rows - FW :], "tile", up)
    after = lax.ppermute(noise[:, :FW], "tile", down)
    halo = jnp.concatenate([before, after], axis=1).reshape(planes * 2 * FW, length)
    blocks = filter_planes(noise, halo, filter_weights(planes, rows))
    got = lax.all_to_all(blocks, "tile", split_axis=0, concat_axis=0, tiled=True)
    got = got.reshape((groups, tiles // groups) + blocks.shape[1:])
    got = lax.all_to_all(got, "grp", split_axis=0, concat_axis=0, tiled=True)
    got = got.reshape((groups, tiles // groups // 2, 2) + blocks.shape[1:])
    inflow, result = march_cells(got, stress, timescale, mean_inflow, courant, prior_state, field)
    return (inflow, result)


def solution(mesh):
    placed = (
        P("grp", None, "tile", None),
        P(None, "tile", "grp"),
        P("tile", "grp"),
        P("tile", "grp"),
        P("tile", "grp"),
        P(None, "tile", "grp"),
        P(None, None, "tile", "grp"),
    )
    return jax.shard_map(
        body,
        mesh=mesh,
        in_specs=placed,
        out_specs=(P(None, None, "tile", "grp"), P(None, None, "tile", "grp")),
        check_vma=False,
    )
```

time: 313 us -> 127 us (0.41); the launches traced: 307 us -> 127 us
  local copies, waits for them, and re-layouts: 105 us -> 5.88 us
  other arithmetic: 97.3 us -> 0.2 us
  blocking collectives: 47.9 us -> 90 us
  waiting for transfers between devices: 35.6 us -> 5.06 us
  Pallas kernels: 0 us -> 18.5 us
  matrix products: 6.73 us -> 0 us
  starting transfers between devices: 13.2 us -> 6.5 us
    unnamed x22 -> x20, local copies, waits for them, and re-layouts: 48.3 us -> 4.56 us
    add x32 -> x0, other arithmetic: 42.5 us -> none  [the longest x16 22.1 us: march(): return (1.0 - courant) * current + courant * upstream]
    all_to_all x1 -> x2, blocking collectives: 47.9 us -> 90 us  [the longest x1 47.6 us: body(): lax.all_to_all(blocks, 'tile', split_axis=0, concat_axis=0, tiled=True)]
    all_to_all x1 -> x0, waiting for transfers between devices: 31.4 us -> none  [body(): lax.all_to_all(lax.all_to_all(flipped, 'tile', split_axis=2, concat_axis=...]
    all_to_all x3 -> x0, local copies, waits for them, and re-layouts: 29.5 us -> none  [the longest x2 21.3 us: body(): lax.all_to_all(flipped, 'tile', split_axis=2, concat_axis=3, tiled=True)]
    another operation x16 -> x0, other arithmetic: 22.1 us -> none  [velocity_of(): jnp.stack([mean_inflow + first_diag * state[0], second_low * state[0] + s...]
    pallas_call x0 -> x2, Pallas kernels: none -> 18.5 us  [the longest x1 11.4 us: filter_planes(): pl.pallas_call(filter_kernel, grid=(windows,), in_specs=[pl.BlockSpec((pl...]
    sub x18 -> x0, other arithmetic: 14.6 us -> none  [the longest x16 14.6 us: march(): return (1.0 - courant) * current + courant * upstream]
  transfers between devices with their start and end apart: 5 -> 2, of which waited for: 4 -> 2; matrix products, arithmetic and copies ran while one was open for 2% -> 0% of each run, Pallas kernels for 0% -> 0%
where the time goes in v1:
time: 127 us
  blocking collectives  90 us (71%)
  Pallas kernels  18.5 us (15%)
  starting transfers between devices  6.5 us (5%)
  local copies, waits for them, and re-layouts  5.88 us (5%)
  waiting for transfers between devices  5.06 us (4%)
    all_to_all x1, blocking collectives, body(): lax.all_to_all(blocks, 'tile', split_axis=0, concat_axis=0, tiled=True)  47.6 us
    all_to_all x1, blocking collectives, body(): got = lax.all_to_all(got, 'grp', split_axis=0, concat_axis=0, tiled=True)  42.4 us
    pallas_call x1, Pallas kernels, filter_planes(): pl.pallas_call(filter_kernel, grid=(windows,), in_specs=[pl.BlockSpec((pl...  11.4 us
    pallas_call x1, Pallas kernels, march_cells(): pl.pallas_call(chain_kernel, grid=(depth // rows,), in_specs=[pl.BlockSpe...  7.16 us
    ppermute x1, starting transfers between devices, body(): before = lax.ppermute(noise[:, rows - FW:], 'tile', up)  4.58 us
    unnamed x20, local copies, waits for them, and re-layouts  4.56 us
    ppermute x1, waiting for transfers between devices, body(): after = lax.ppermute(noise[:, :FW], 'tile', down)  4.4 us
  transfers between devices with their start and end apart: 2, of which 2 were waited for; matrix products, arithmetic and copies ran while one was open for 0% of the time, Pallas kernels for 0%

profile of v1, /device:TPU:1, one launch (start us, length us, event | category | flops | bytes accessed | tf_op | source)
XLA Modules:
  0.0 126.8 jit_solution(11602867900414542049)
XLA Ops:
  0.6 1.3 %fusion = (bf16[12,4,2048]{2,1,0:T(4,128)(2,1)S(1)}, bf16[12,4,2048]{2,1,0:T(4,128)(2,1)S(1)}) fusion(bf16[12,64,2048]{2,1,0:T(8,128)(2,1)} %bitcast.5), kind=kLoop, calls=%fused_computation.1 | loop fusion | bytes 786432 | tf_op jit(solution)/shard_map/slice | solution.py:201
  2.0 4.6 %collective-permute-start = (bf16[12,4,2048]{2,1,0:T(4,128)(2,1)S(1)}, bf16[12,4,2048]{2,1,0:T(4,128)(2,1)S(1)}, u32[]{:S(2)}, u32[]{:S(2)}) collective-permute-start(bf16[12,4,2048]{2,1,0:T(4,128)(2,1)S(1)} %get-tuple-element.2), channel_id=1, source_target_pairs={{0,1},{1,2},{2,3},{3,4},{4,5},{5,6},{6,7},{7,8},{8,9},{9,10},{10,1... | collective-permute-start | bytes 589832 | tf_op jit(solution)/shard_map/ppermute | solution.py:201
  6.5 1.9 %collective-permute-start.1 = (bf16[12,4,2048]{2,1,0:T(4,128)(2,1)S(1)}, bf16[12,4,2048]{2,1,0:T(4,128)(2,1)S(1)}, u32[]{:S(2)}, u32[]{:S(2)}) collective-permute-start(bf16[12,4,2048]{2,1,0:T(4,128)(2,1)S(1)} %get-tuple-element.3), channel_id=1, source_target_pairs={{1,0},{2,1},{3,2},{4,3},{5,4},{6,5},{7,6},{8,7},{9,8},{10,9},{11,1... | collective-permute-start | bytes 589832 | tf_op jit(solution)/shard_map/ppermute | solution.py:202
  8.5 0.7 collective-permute-done
  9.1 4.4 %collective-permute-done.1 = bf16[12,4,2048]{2,1,0:T(4,128)(2,1)S(1)} collective-permute-done((bf16[12,4,2048]{2,1,0:T(4,128)(2,1)S(1)}, bf16[12,4,2048]{2,1,0:T(4,128)(2,1)S(1)}, u32[]{:S(2)}, u32[]{:S(2)}) %collective-permute-start.1) | collective-permute-done | bytes 196640 | tf_op jit(solution)/shard_map/ppermute | solution.py:202
  13.5 0.2 maximum_bitcast_fusion.hleft_ref.hright_ref
  13.7 0.0 copy-start
  13.7 1.9 %copy-done = bf16[4,3,64,2048]{3,2,1,0:T(8,128)(2,1)S(1)} copy-done((bf16[4,3,64,2048]{3,2,1,0:T(8,128)(2,1)S(1)}, bf16[4,3,64,2048]{3,2,1,0:T(8,128)(2,1)}, u32[]{:S(2)}) %copy-start) | copy-done | bytes 3145752
  15.6 0.0 copy-start.4
  15.6 0.9 copy-done.4
  16.5 0.0 copy-start.8
  16.5 0.9 copy-done.8
  17.4 0.0 copy-start.9
  17.4 0.8 copy-done.9
  18.3 11.4 %filter.1 = bf16[32,6,64,128]{3,2,1,0:T(8,128)(2,1)S(1)} custom-call(bf16[12,64,2048]{2,1,0:T(8,128)(2,1)S(1)} %bitcast.6, bf16[12,64,2048]{2,1,0:T(8,128)(2,1)S(1)} %bitcast.7, bf16[96,2048]{1,0:T(8,128)(2,1)S(1)} %maximum_bitcast_fusion.hleft_ref.hright_ref, bf16[96,2048]{1,0:T(8,128)(2,1)S(1)} %maximum_bitcast_fusion.hleft_ref.hright_ref, ...), custom_call_target="tpu_custom_call" | custom-call | tf_op jit(solution)/shard_map/filter/pallas_call | solution.py:74
  29.6 47.6 %all_to_all.10 = bf16[32,6,64,128]{3,2,1,0:T(8,128)(2,1)S(1)} all-to-all(bf16[32,6,64,128]{3,2,1,0:T(8,128)(2,1)S(1)} %filter.1), channel_id=1, replica_groups=mesh['grp'=4,'tile'=32] {'tile'}, dimensions={0} | all-to-all | bytes 6291456 | tf_op jit(solution)/shard_map/all_to_all | solution.py:205
  77.2 0.0 copy-start.1
  77.2 0.0 copy-start.2
  77.2 0.0 copy-start.3
  77.2 0.0 copy-start.5
  77.2 0.0 copy-start.6
  77.3 0.0 copy-start.7
  77.3 42.4 %all_to_all.11 = bf16[4,8,6,64,128]{4,3,2,1,0:T(8,128)(2,1)S(1)} all-to-all(bf16[4,8,6,64,128]{4,3,2,1,0:T(8,128)(2,1)S(1)} %bitcast.9), channel_id=1, replica_groups=mesh['grp'=4,'tile'=32] {'grp'}, dimensions={0} | all-to-all | bytes 6291456 | tf_op jit(solution)/shard_map/all_to_all | solution.py:207
  119.6 0.0 copy-done.1
  119.6 0.0 copy-done.2
  119.6 0.0 copy-done.3
  119.6 0.0 copy-done.5
  119.7 0.0 copy-done.6
  119.7 0.0 copy-done.7
  119.7 7.2 %march.1 = (bf16[16,3,64,512]{3,2,1,0:T(8,128)(2,1)}, f32[3,8,64,512]{3,2,1,0:T(8,128)}) custom-call(bf16[4,4,2,6,64,128]{5,4,3,2,1,0:T(8,128)(2,1)S(1)} %bitcast.8, f32[6,64,512]{2,1,0:T(8,128)S(1)} %copy-done.2, f32[64,512]{1,0:T(8,128)S(1)} %copy-done.5, f32[64,512]{1,0:T(8,128)S(1)} %copy-done.6, f32[64,512]{1,0:T(8,128)S(1)} %copy-done.7, ...), custom_call_target="tpu_custom_call" | custom-call | tf_op jit(solution)/shard_map/march/pallas_call | solution.py:171
Async XLA Ops:
  2.0 7.2 %collective-permute-start = (bf16[12,4,2048]{2,1,0:T(4,128)(2,1)S(1)}, bf16[12,4,2048]{2,1,0:T(4,128)(2,1)S(1)}, u32[]{:S(2)}, u32[]{:S(2)}) collective-permute-start(bf16[12,4,2048]{2,1,0:T(4,128)(2,1)S(1)} %get-tuple-element.2), channel_id=1, source_target_pairs={{0,1},{1,2},{2,3},{3,4},{4,5},{5,6},{6,7},{7,8},{8,9},{9,10},{10,1... | collective-permute-start | bytes 589832 | tf_op jit(solution)/shard_map/ppermute | solution.py:201
  6.5 7.0 %collective-permute-start.1 = (bf16[12,4,2048]{2,1,0:T(4,128)(2,1)S(1)}, bf16[12,4,2048]{2,1,0:T(4,128)(2,1)S(1)}, u32[]{:S(2)}, u32[]{:S(2)}) collective-permute-start(bf16[12,4,2048]{2,1,0:T(4,128)(2,1)S(1)} %get-tuple-element.3), channel_id=1, source_target_pairs={{1,0},{2,1},{3,2},{4,3},{5,4},{6,5},{7,6},{8,7},{9,8},{10,9},{11,1... | collective-permute-start | bytes 589832 | tf_op jit(solution)/shard_map/ppermute | solution.py:202
  13.7 1.9 %copy-start = (bf16[4,3,64,2048]{3,2,1,0:T(8,128)(2,1)S(1)}, bf16[4,3,64,2048]{3,2,1,0:T(8,128)(2,1)}, u32[]{:S(2)}) copy-start(bf16[4,3,64,2048]{3,2,1,0:T(8,128)(2,1)} %param.10) | copy-start | bytes 9437188
  15.6 0.9 copy-start.4
  16.5 0.9 copy-start.8
  17.4 0.8 copy-start.9
  77.2 42.4 %copy-start.1 = (f32[3,8,64,512]{3,2,1,0:T(8,128)S(1)}, f32[3,8,64,512]{3,2,1,0:T(8,128)}, u32[]{:S(2)}) copy-start(f32[3,8,64,512]{3,2,1,0:T(8,128)} %field_ref.1) | copy-start | bytes 9437188
  77.2 42.4 %copy-start.2 = (f32[6,64,512]{2,1,0:T(8,128)S(1)}, f32[6,64,512]{2,1,0:T(8,128)}, u32[]{:S(2)}) copy-start(f32[6,64,512]{2,1,0:T(8,128)} %stress_ref.1) | copy-start | bytes 2359300
  77.2 42.4 %copy-start.3 = (f32[3,64,512]{2,1,0:T(8,128)S(1)}, f32[3,64,512]{2,1,0:T(8,128)}, u32[]{:S(2)}) copy-start(f32[3,64,512]{2,1,0:T(8,128)} %prior_ref.1) | copy-start | bytes 1179652
  77.2 42.4 %copy-start.5 = (f32[64,512]{1,0:T(8,128)S(1)}, f32[64,512]{1,0:T(8,128)}, u32[]{:S(2)}) copy-start(f32[64,512]{1,0:T(8,128)} %timescale_ref.1) | copy-start | bytes 393220
  77.2 42.4 %copy-start.6 = (f32[64,512]{1,0:T(8,128)S(1)}, f32[64,512]{1,0:T(8,128)}, u32[]{:S(2)}) copy-start(f32[64,512]{1,0:T(8,128)} %mean_ref.1) | copy-start | bytes 393220
  77.3 42.4 %copy-start.7 = (f32[64,512]{1,0:T(8,128)S(1)}, f32[64,512]{1,0:T(8,128)}, u32[]{:S(2)}) copy-start(f32[64,512]{1,0:T(8,128)} %courant_ref.1) | copy-start | bytes 393220
